TPU v7x, 32 devices: a 4x4x1 block of a 4x4x8 slice. The times are simulated.
32 devices in a mesh: dp: 1 (over z), ep: 32 (over y, x, core).
Axes of the slice: x: 4, y: 4, z: 1, core: 2. Of those that a mesh axis runs over, the one named last changes fastest.
The devices are a block of a 4x4x8 slice.
Arguments:
- tokens: bfloat16 [32, 1024, 768], P(('dp', 'ep'))
- w_gate: bfloat16 [768, 64], replicated
- expert_ids: int32 [32, 1024, 2], P(('dp', 'ep'))
- keep_second: int32 [32, 1024], P(('dp', 'ep'))
- w_in: bfloat16 [64, 768, 3072], P('ep')
- w_out: bfloat16 [64, 3072, 768], P('ep')
Outputs:
- output: bfloat16 [32, 1024, 768], P(('dp', 'ep'))
All inputs are finite; a program needn't handle non-finite values.
Results may differ from a plain program's by a relative error of at most 0.001.
Values are sent between devices in bfloat16 or wider.
A program may use at most 768 MiB of HBM per device.

v0:
```python
import jax
import jax.numpy as jnp
from jax import lax
from jax.sharding import PartitionSpec as P


def build_routing(tokens, w_gate, expert_ids, keep_second, capacity):
    expert_count = w_gate.shape[1]
    logits = jnp.einsum("gsm,me->gse", tokens, w_gate, preferred_element_type=jnp.float32)
    gate_probs = jax.nn.softmax(logits, axis=-1)
    first_hot = jax.nn.one_hot(expert_ids[:, :, 0], expert_count, dtype=jnp.int32)
    second_hot = jax.nn.one_hot(expert_ids[:, :, 1], expert_count, dtype=jnp.int32) * keep_second[:, :, None]
    gate_first = jnp.sum(gate_probs * first_hot, axis=-1)
    gate_second = jnp.sum(gate_probs * second_hot, axis=-1)
    gate_total = gate_first + gate_second
    pos_first = jnp.sum((jnp.cumsum(first_hot, axis=1) - first_hot) * first_hot, axis=-1)
    second_base = jnp.cumsum(second_hot, axis=1) - second_hot + jnp.sum(first_hot, axis=1, keepdims=True)
    pos_second = jnp.sum(second_base * second_hot, axis=-1)
    slot_first = first_hot.astype(jnp.bfloat16)[:, :, :, None] * jax.nn.one_hot(pos_first, capacity, dtype=jnp.bfloat16)[:, :, None, :]
    slot_second = second_hot.astype(jnp.bfloat16)[:, :, :, None] * jax.nn.one_hot(pos_second, capacity, dtype=jnp.bfloat16)[:, :, None, :]
    dispatch = slot_first + slot_second
    weight_first = (gate_first / gate_total).astype(jnp.bfloat16)[:, :, None, None]
    weight_second = (gate_second / gate_total).astype(jnp.bfloat16)[:, :, None, None]
    combine = weight_first * slot_first + weight_second * slot_second
    return dispatch, combine


def solution(mesh):
    group_count = mesh.shape["ep"]

    def local_layer(tokens, w_gate, expert_ids, keep_second, w_in, w_out):
        token_count = tokens.shape[1]
        model_dim = tokens.shape[2]
        expert_count = w_gate.shape[1]
        local_experts = w_in.shape[0]
        capacity = 2 * token_count // expert_count
        dispatch, combine = build_routing(tokens, w_gate, expert_ids, keep_second, capacity)
        send_rows = jnp.einsum("gsec,gsm->ecm", dispatch, tokens, preferred_element_type=jnp.float32).astype(jnp.bfloat16)
        send_rows = send_rows.reshape(group_count, local_experts, capacity, model_dim)
        recv_rows = lax.all_to_all(send_rows, "ep", 0, 0, tiled=True)
        hidden = jax.nn.relu(jnp.einsum("gecm,emh->egch", recv_rows, w_in, preferred_element_type=jnp.float32)).astype(jnp.bfloat16)
        back_rows = jnp.einsum("egch,ehm->gecm", hidden, w_out, preferred_element_type=jnp.float32).astype(jnp.bfloat16)
        back_rows = lax.all_to_all(back_rows, "ep", 0, 0, tiled=True)
        back_rows = back_rows.reshape(expert_count, capacity, model_dim)
        mixed_rows = jnp.einsum("gsec,ecm->gsm", combine, back_rows, preferred_element_type=jnp.float32)
        return mixed_rows.astype(jnp.bfloat16)

    group_spec = P(("dp", "ep"))
    return jax.shard_map(local_layer, mesh=mesh, in_specs=(group_spec, P(), group_spec, group_spec, P("ep"), P("ep")), out_specs=group_spec, check_vma=False)
```

profile of v0, /device:TPU:97, one launch (start us, length us, event | category | flops | bytes accessed | tf_op | source)
XLA Modules:
  0.0 179.3 jit_solution(14404107879894784272)
XLA Ops:
  0.0 0.9 fusion.57
  0.9 0.7 select_convert_fusion
  1.6 0.7 select_bitcast_fusion
  2.4 18.0 %reduce-window.16 = s32[1,64,8,128]{3,2,1,0:T(8,128)S(1)} reduce-window(s32[1,64,8,128]{3,2,1,0:T(8,128)S(1)} %bitcast.64, s32[]{:T(128)} %constant.14.clone.1), window={size=1x1x1x128 pad=0_0x0_0x0_0x127_0}, to_apply=%region_7.8 | reduce-window | flops 8323072 | bytes 524292 | tf_op jit(solution)/shard_map/reduce-window.2
  20.4 0.1 slice.26
  20.7 18.0 %reduce-window.14 = s32[1,64,8,128]{3,2,1,0:T(8,128)S(1)} reduce-window(s32[1,64,8,128]{3,2,1,0:T(8,128)S(1)} %bitcast.65, s32[]{:T(128)} %constant.14.clone.1), window={size=1x1x1x128 pad=0_0x0_0x0_0x127_0}, to_apply=%region_4.5 | reduce-window | flops 8323072 | bytes 524292 | tf_op jit(solution)/shard_map/reduce-window
  38.7 0.1 slice.24
  38.9 0.1 copy.25
  39.1 0.1 copy.26
  39.1 0.1 broadcast.221
  39.3 0.1 copy.23
  39.6 0.1 broadcast.219
  39.8 0.2 fusion.43
  40.0 0.1 fusion.49
  40.1 0.6 multiply_add_fusion
  40.7 4.8 %fusion.15 = bf16[64,32,768]{2,1,0:T(8,128)(2,1)S(1)} fusion(bf16[1024,64,32]{0,1,2:T(8,128)(2,1)S(1)} %multiply_add_fusion, bf16[1,1024,768]{2,1,0:T(8,128)(2,1)S(1)} %copy-done), kind=kOutput, calls=%fused_computation.17 | convolution fusion | flops 3222798336 | bytes 8912896 | tf_op jit(solution)/shard_map/gsec,gsm->ecm/dot_general | solution.py:38
  45.6 51.1 %all_to_all.10 = bf16[32,2,32,768]{3,2,1,0:T(8,128)(2,1)} all-to-all(bf16[32,2,32,768]{3,2,1,0:T(8,128)(2,1)S(1)} %bitcast.63), channel_id=1, replica_groups=mesh['dp'=1,'ep'=32] {'ep'}, dimensions={0} | all-to-all | bytes 6291456 | tf_op jit(solution)/shard_map/all_to_all | solution.py:40
  96.6 25.4 %convert_bitcast_fusion = bf16[32,2,32,768]{3,2,0,1:T(8,128)(2,1)} fusion(bf16[2,3072,768]{2,1,0:T(8,128)(2,1)} %param.11, bf16[2,768,3072]{2,1,0:T(8,128)(2,1)} %param.10, bf16[32,2,32,768]{3,2,1,0:T(8,128)(2,1)} %all_to_all.10), kind=kOutput, calls=%fused_computation.16 | convolution fusion | flops 19341508608 | bytes 25165824 | tf_op jit(solution)/shard_map/egch,ehm->gecm/dot_general | solution.py:42
  122.1 3.9 %copy.29 = bf16[32,2,32,768]{3,2,1,0:T(8,128)(2,1)} copy(bf16[32,2,32,768]{3,2,0,1:T(8,128)(2,1)} %convert_bitcast_fusion) | data formatting | bytes 6291456 | tf_op jit(solution)/shard_map/convert_element_type | solution.py:42
  125.9 4.1 %all-to-all-start.1 = ((bf16[32,2,32,768]{3,2,1,0:T(8,128)(2,1)}), bf16[32,2,32,768]{3,2,1,0:T(8,128)(2,1)}, u32[]{:S(2)}, u32[]{:S(2)}) async-start(bf16[32,2,32,768]{3,2,1,0:T(8,128)(2,1)} %copy.29), calls=%async_computation.1 | async-start | bytes 6291456 | tf_op jit(solution)/shard_map/all_to_all | solution.py:43
  130.0 0.6 fusion.58
  130.7 0.1 fusion.47
  130.8 36.9 %all-to-all-done.1 = bf16[32,2,32,768]{3,2,1,0:T(8,128)(2,1)} async-done(((bf16[32,2,32,768]{3,2,1,0:T(8,128)(2,1)}), bf16[32,2,32,768]{3,2,1,0:T(8,128)(2,1)}, u32[]{:S(2)}, u32[]{:S(2)}) %all-to-all-start.1) | async-done | bytes 3145760 | tf_op jit(solution)/shard_map/all_to_all | solution.py:43
  167.8 11.6 %fusion.37 = bf16[1,1024,768]{2,1,0:T(8,128)(2,1)} fusion(bf16[64,32,768]{2,1,0:T(8,128)(2,1)} %bitcast.19, bf16[1024,32]{0,1:T(8,128)(2,1)S(1)} %get-tuple-element.16, bf16[1024,64]{0,1:T(8,128)(2,1)S(1)} %select_convert_fusion, bf16[1024]{0:T(1024)(128)(2,1)S(1)} %get-tuple-element.10, bf16[1024,32]{0,1:T(8,128)(2,1)S(1)} %get-tuple-element.15, ...), kind=kOutput, calls=%fused_computation.27 | convolution fusion | flops 3232497664 | bytes 5115904 | tf_op jit(solution)/shard_map/gsec,ecm->gsm/dot_general | solution.py:45
  (22 shorter events, 0.6 us)
Async XLA Ops:
  0.0 40.7 %copy-start = (bf16[1,1024,768]{2,1,0:T(8,128)(2,1)S(1)}, bf16[1,1024,768]{2,1,0:T(8,128)(2,1)}, u32[]{:S(2)}) copy-start(bf16[1,1024,768]{2,1,0:T(8,128)(2,1)} %param.6) | copy-start | bytes 4718596
  0.0 40.0 %copy-start.2 = (s32[1,1024]{1,0:T(1,128)S(1)}, s32[1,1024]{1,0:T(1,128)}, u32[]{:S(2)}) copy-start(s32[1,1024]{1,0:T(1,128)} %param.9) | copy-start | bytes 12292
  125.9 4.1 %copy-start.1 = (bf16[768,64]{0,1:T(8,128)(2,1)S(1)}, bf16[768,64]{0,1:T(8,128)(2,1)}, u32[]{:S(2)}) copy-start(bf16[768,64]{0,1:T(8,128)(2,1)} %param.7) | copy-start | bytes 294916
  125.9 41.8 %all-to-all-start.1 = ((bf16[32,2,32,768]{3,2,1,0:T(8,128)(2,1)}), bf16[32,2,32,768]{3,2,1,0:T(8,128)(2,1)}, u32[]{:S(2)}, u32[]{:S(2)}) async-start(bf16[32,2,32,768]{3,2,1,0:T(8,128)(2,1)} %copy.29), calls=%async_computation.1 | async-start | bytes 6291456 | tf_op jit(solution)/shard_map/all_to_all | solution.py:43
where the time goes:
time: 182 us; the launch traced here: 179 us
  blocking collectives  51.1 us (28%)
  matrix products  42.4 us (23%)
  other arithmetic  38.7 us (21%)
  waiting for transfers between devices  36.9 us (20%)
  local copies, waits for them, and re-layouts  5.99 us (3%)
  starting transfers between devices  4.08 us (2%)
    all_to_all x1, blocking collectives, local_layer(): recv_rows = lax.all_to_all(send_rows, 'ep', 0, 0, tiled=True)  51.1 us
    all_to_all x1, waiting for transfers between devices, local_layer(): back_rows = lax.all_to_all(back_rows, 'ep', 0, 0, tiled=True)  36.9 us
    another operation x4, other arithmetic  36.1 us
    dot_general x1, matrix products, local_layer(): jnp.einsum('egch,ehm->gecm', hidden, w_out, preferred_element_type=jnp.fl...  25.4 us
    dot_general x1, matrix products, local_layer(): jnp.einsum('gsec,ecm->gsm', combine, back_rows, preferred_element_type=jn...  11.6 us
    dot_general x1, matrix products, local_layer(): jnp.einsum('gsec,gsm->ecm', dispatch, tokens, preferred_element_type=jnp....  4.81 us
    all_to_all x1, starting transfers between devices, local_layer(): back_rows = lax.all_to_all(back_rows, 'ep', 0, 0, tiled=True)  4.08 us
    convert_element_type x1, local copies, waits for them, and re-layouts, local_layer(): jnp.einsum('egch,ehm->gecm', hidden, w_out, preferred_element_type=jnp.fl...  3.88 us
  transfers between devices with their start and end apart: 1, of which 1 were waited for; matrix products, arithmetic and copies ran while one was open for 0% of the time, Pallas kernels for 0%

commit v1 on v0

v1 whole, which is shorter than its diff:
```python
import functools
import math

import jax
import jax.numpy as jnp
from jax import lax
from jax.experimental import pallas as pl
from jax.experimental.pallas import tpu as pltpu
from jax.sharding import PartitionSpec as P

F32 = jnp.float32
BF16 = jnp.bfloat16
MESH = pl.DeviceIdType.MESH
CHUNK = 8


def step_offsets(side):
    hop = lambda d: min(d, side - d)
    chips = [(dy, dx) for dy in range(side) for dx in range(side)]
    kinds = [(2, 1), (1, 1), (2, 2), (2, 0), (0, 0), (1, 0)]
    order = []
    for kind in kinds:
        same = [c for c in chips if tuple(sorted((hop(c[0]), hop(c[1])), reverse=True)) == kind]
        order += [(dy, dx, core) for core in range(2) for (dy, dx) in same]
    return order


def layer_kernel(
    n, offsets, tok_hbm, wg_hbm, ids_hbm, keep_hbm, wi_hbm, wo_hbm, out_ref,
    tok, wg, ids, keep, wi, wo, onehot, send, recv, back, home, cols, cw, acc,
    local_sem, fs_sem, fr_sem, bs_sem, br_sem,
):
    side = math.isqrt(n // 2)
    token_count, model_dim = tok.shape
    expert_count = wg.shape[0]
    local_experts, _, hidden_dim = wi.shape
    steps, rows, _ = send.shape
    capacity = rows // local_experts
    chunks = steps // CHUNK
    span = CHUNK * rows
    self_step = offsets.index((0, 0, 0))

    loads = [
        pltpu.make_async_copy(src, dst, local_sem.at[i])
        for i, (src, dst) in enumerate([(ids_hbm, ids), (keep_hbm, keep), (tok_hbm, tok), (wg_hbm, wg)])
    ]
    for e in range(local_experts):
        loads.append(pltpu.make_async_copy(wi_hbm.at[e], wi.at[e], local_sem.at[4 + 2 * e]))
        loads.append(pltpu.make_async_copy(wo_hbm.at[e], wo.at[e], local_sem.at[5 + 2 * e]))
    for load in loads[:4]:
        load.start()

    barrier = pltpu.get_barrier_semaphore()

    @pl.loop(0, n)
    def _(k):
        pl.semaphore_signal(barrier, inc=1, device_id={"ep": k}, device_id_type=MESH)

    me = lax.axis_index("ep")
    my_y, my_x, my_core = me // (2 * side), (me // 2) % side, me % 2

    def peer(step, sign):
        dy, dx, core = offsets[step]
        y, x = (my_y + sign * dy + side) % side, (my_x + sign * dx + side) % side
        return (y * side + x) * 2 + (my_core + core) % 2

    dst = [peer(k, 1) for k in range(steps)]
    src = [peer(k, -1) for k in range(steps)]

    def remote(buf_from, buf_to, ssem, rsem, k, device):
        return pltpu.make_async_remote_copy(
            src_ref=buf_from.at[k], dst_ref=buf_to.at[k], send_sem=ssem.at[k], recv_sem=rsem.at[k],
            device_id={"ep": device}, device_id_type=MESH)

    forth = [remote(send, recv, fs_sem, fr_sem, k, dst[k]) for k in range(steps)]
    home_copy = [remote(back, home, bs_sem, br_sem, k, src[k]) for k in range(steps)]

    loads[0].wait()
    loads[1].wait()
    first_id, second_id = ids[0:1, :], ids[1:2, :]
    used = keep[...] == 1
    expert_row = lax.broadcasted_iota(jnp.int32, (expert_count, token_count), 0)
    first_hot = jnp.where(expert_row == first_id, 1.0, 0.0).astype(F32)
    second_hot = jnp.where((expert_row == second_id) & used, 1.0, 0.0).astype(F32)
    first_total = jnp.sum(first_hot, axis=1, keepdims=True)
    both = jnp.concatenate([first_hot, second_hot], axis=0)
    both16 = both.astype(BF16)
    width = 256
    before = jnp.where(
        lax.broadcasted_iota(jnp.int32, (width, width), 0) < lax.broadcasted_iota(jnp.int32, (width, width), 1),
        1.0, 0.0).astype(BF16)
    carry = jnp.concatenate([jnp.zeros((expert_count, 1), F32), first_total], axis=0)
    pos = []
    for b in range(token_count // width):
        part = both[:, b * width:(b + 1) * width]
        ahead = jnp.dot(both16[:, b * width:(b + 1) * width], before, preferred_element_type=F32) + carry
        picked = part * ahead
        pos.append((jnp.sum(picked[:expert_count], axis=0, keepdims=True), jnp.sum(picked[expert_count:], axis=0, keepdims=True)))
        carry = carry + jnp.sum(part, axis=1, keepdims=True)
    pos_first = jnp.concatenate([p[0] for p in pos], axis=1).astype(jnp.int32)
    pos_second = jnp.concatenate([p[1] for p in pos], axis=1).astype(jnp.int32)
    slot_first = jnp.where(pos_first < capacity, first_id * capacity + pos_first, -1)
    slot_second = jnp.where(used & (pos_second < capacity), second_id * capacity + pos_second, -1)

    loads[2].wait()
    for c in range(chunks):
        for j in range(CHUNK):
            slot = dst[c * CHUNK + j] * rows + lax.broadcasted_iota(jnp.int32, (rows, token_count), 0)
            hit = (slot == slot_first) | (slot == slot_second)
            onehot[j * rows:(j + 1) * rows, :] = jnp.where(hit, 1.0, 0.0).astype(BF16)
        for col in range(0, model_dim, width):
            picked = jnp.dot(onehot[...], tok[:, col:col + width], preferred_element_type=F32).astype(BF16)
            for j in range(CHUNK):
                k = c * CHUNK + j
                target = recv if k == self_step else send
                target[k, :, col:col + width] = picked[j * rows:(j + 1) * rows]
        if c == 0:
            pl.semaphore_wait(barrier, n)
        for k in range(c * CHUNK, (c + 1) * CHUNK):
            if k != self_step:
                forth[k].start()
        if c == 0:
            for load in loads[4:]:
                load.start()

    loads[3].wait()
    logits = lax.dot_general(wg[...], tok[...], (((1,), (1,)), ((), ())), preferred_element_type=F32)
    top = jnp.max(logits, axis=0, keepdims=True)
    raised = jnp.exp(logits - top)
    probs = raised / jnp.sum(raised, axis=0, keepdims=True)
    expert_row = lax.broadcasted_iota(jnp.int32, (expert_count, token_count), 0)
    gate_first = jnp.sum(jnp.where(expert_row == first_id, probs, 0.0), axis=0, keepdims=True)
    gate_second = jnp.sum(jnp.where((expert_row == second_id) & used, probs, 0.0), axis=0, keepdims=True)
    gate_total = gate_first + gate_second
    lines = jnp.concatenate(
        [slot_first.astype(F32), slot_second.astype(F32), gate_first / gate_total, gate_second / gate_total,
         jnp.zeros((124, token_count), F32)], axis=0)
    cols[...] = jnp.transpose(lines)
    block = 64
    for c in range(chunks):
        lane = lax.broadcasted_iota(jnp.int32, (1, span), 1)
        slot = lane % rows
        for j in range(CHUNK):
            slot = slot + jnp.where(lane // rows == j, dst[c * CHUNK + j] * rows, 0)
        slot = slot.astype(F32)

        @pl.loop(0, token_count // block)
        def _(i):
            r = pl.ds(pl.multiple_of(i * block, block), block)
            line = cols[r, :]
            weight = jnp.where(line[:, 0:1] == slot, line[:, 2:3], 0.0) + jnp.where(line[:, 1:2] == slot, line[:, 3:4], 0.0)
            cw[r, c * span:(c + 1) * span] = weight.astype(BF16)

    for load in loads[4:]:
        load.wait()
    for c in range(chunks):
        for k in range(c * CHUNK, (c + 1) * CHUNK):
            if k != self_step:
                forth[k].wait_recv()

        @pl.loop(0, local_experts)
        def _(e):
            r = pl.ds(pl.multiple_of(e * capacity, capacity), capacity)
            x = recv[c * CHUNK:(c + 1) * CHUNK, r, :].reshape(CHUNK * capacity, model_dim)
            y = jnp.zeros((CHUNK * capacity, model_dim), F32)
            tile = 768
            for h in range(0, hidden_dim, tile):
                hidden = jnp.dot(x, wi[e, :, h:h + tile], preferred_element_type=F32)
                hidden = jnp.maximum(hidden, 0.0).astype(BF16)
                y = y + jnp.dot(hidden, wo[e, h:h + tile, :], preferred_element_type=F32)
            y = y.astype(BF16).reshape(CHUNK, capacity, model_dim)
            back[c * CHUNK:(c + 1) * CHUNK, r, :] = y
            if self_step // CHUNK == c:
                home[self_step, r, :] = y[self_step % CHUNK]

        for k in range(c * CHUNK, (c + 1) * CHUNK):
            if k != self_step:
                home_copy[k].start()

    block = 256
    for c in range(chunks):
        for k in range(c * CHUNK, (c + 1) * CHUNK):
            if k != self_step:
                home_copy[k].wait_recv()

        @pl.loop(0, token_count // block)
        def _(i):
            r = pl.ds(pl.multiple_of(i * block, block), block)
            y = home[c * CHUNK:(c + 1) * CHUNK].reshape(span, model_dim)
            part = jnp.dot(cw[r, c * span:(c + 1) * span], y, preferred_element_type=F32)
            if c > 0:
                part = acc[r, :] + part
            if c < chunks - 1:
                acc[r, :] = part
            else:
                out_ref[r, :] = part.astype(BF16)

    for k in range(steps):
        if k != self_step:
            forth[k].wait_send()
            home_copy[k].wait_send()


def solution(mesh):
    n = mesh.shape["ep"]
    offsets = step_offsets(math.isqrt(n // 2))

    def local_layer(tokens, w_gate, expert_ids, keep_second, w_in, w_out):
        token_count, model_dim = tokens.shape[1:]
        expert_count = w_gate.shape[1]
        local_experts, _, hidden_dim = w_in.shape
        capacity = 2 * token_count // expert_count
        rows = local_experts * capacity
        any_space = pl.BlockSpec(memory_space=pl.ANY)
        vmem = pltpu.VMEM
        out = pl.pallas_call(
            functools.partial(layer_kernel, n, offsets),
            out_shape=jax.ShapeDtypeStruct((token_count, model_dim), BF16),
            in_specs=[any_space] * 6,
            out_specs=pl.BlockSpec(memory_space=vmem),
            scratch_shapes=[
                vmem((token_count, model_dim), BF16),
                vmem((expert_count, model_dim), BF16),
                vmem((2, token_count), jnp.int32),
                vmem((1, token_count), jnp.int32),
                vmem(w_in.shape, BF16),
                vmem(w_out.shape, BF16),
                vmem((CHUNK * rows, token_count), BF16),
                vmem((n, rows, model_dim), BF16),
                vmem((n, rows, model_dim), BF16),
                vmem((n, rows, model_dim), BF16),
                vmem((n, rows, model_dim), BF16),
                vmem((token_count, 128), F32),
                vmem((token_count, n * rows), BF16),
                vmem((token_count, model_dim), F32),
                pltpu.SemaphoreType.DMA((4 + 2 * local_experts,)),
                pltpu.SemaphoreType.DMA((n,)),
                pltpu.SemaphoreType.DMA((n,)),
                pltpu.SemaphoreType.DMA((n,)),
                pltpu.SemaphoreType.DMA((n,)),
            ],
            compiler_params=pltpu.CompilerParams(
                collective_id=0, has_side_effects=True, vmem_limit_bytes=60 * 1024 * 1024),
            name="moe_layer",
        )(tokens[0], w_gate.T, expert_ids[0].T, keep_second, w_in, w_out)
        return out[None]

    group_spec = P(("dp", "ep"))
    return jax.shard_map(
        local_layer, mesh=mesh, in_specs=(group_spec, P(), group_spec, group_spec, P("ep"), P("ep")),
        out_specs=group_spec, check_vma=False)
```

time: 182 us -> 94.5 us (0.52); the launches traced: 179 us -> 94.4 us
  Pallas kernels: 0 us -> 91.8 us
  blocking collectives: 51.1 us -> 0 us
  matrix products: 42.4 us -> 0 us
  other arithmetic: 38.7 us -> 0 us
  waiting for transfers between devices: 36.9 us -> 0 us
  starting transfers between devices: 4.08 us -> 0 us
  local copies, waits for them, and re-layouts: 5.99 us -> 2.65 us
    pallas_call x0 -> x1, Pallas kernels: none -> 91.8 us  [local_layer(): pl.pallas_call(functools.partial(layer_kernel, n, offsets), out_shape=jax...]
    all_to_all x1 -> x0, blocking collectives: 51.1 us -> none  [local_layer(): recv_rows = lax.all_to_all(send_rows, 'ep', 0, 0, tiled=True)]
    dot_general x4 -> x0, matrix products: 42.4 us -> none  [the longest x1 25.4 us: local_layer(): jnp.einsum('egch,ehm->gecm', hidden, w_out, preferred_element_type=jnp.fl...]
    all_to_all x1 -> x0, waiting for transfers between devices: 36.9 us -> none  [local_layer(): back_rows = lax.all_to_all(back_rows, 'ep', 0, 0, tiled=True)]
    another operation x4 -> x0, other arithmetic: 36.1 us -> none
    all_to_all x1 -> x0, starting transfers between devices: 4.08 us -> none  [local_layer(): back_rows = lax.all_to_all(back_rows, 'ep', 0, 0, tiled=True)]
    convert_element_type x1 -> x0, local copies, waits for them, and re-layouts: 3.88 us -> none  [local_layer(): jnp.einsum('egch,ehm->gecm', hidden, w_out, preferred_element_type=jnp.fl...]
    unnamed x8 -> x1, local copies, waits for them, and re-layouts: 0.11 us -> 2.65 us
  transfers between devices with their start and end apart: 1 -> 0, of which waited for: 1 -> 0; matrix products, arithmetic and copies ran while one was open for 0% -> 0% of each run, Pallas kernels for 0% -> 0%
where the time goes in v1:
time: 94.5 us; the launch traced here: 94.4 us
  Pallas kernels  91.8 us (97%)
  local copies, waits for them, and re-layouts  2.65 us (3%)
    pallas_call x1, Pallas kernels, local_layer(): pl.pallas_call(functools.partial(layer_kernel, n, offsets), out_shape=jax...  91.8 us
    unnamed x1, local copies, waits for them, and re-layouts  2.65 us

profile of v1, /device:TPU:97, one launch (start us, length us, event | category | flops | bytes accessed | tf_op | source)
XLA Modules:
  0.0 94.4 jit_solution(12330462846396161796)
XLA Ops:
  0.0 91.8 %moe_layer.1 = bf16[1024,768]{1,0:T(8,128)(2,1)} custom-call(bf16[1024,768]{1,0:T(8,128)(2,1)} %bitcast.7, bf16[64,768]{1,0:T(8,128)(2,1)} %bitcast.8, s32[2,1024]{1,0:T(2,128)} %bitcast.9, s32[1,1024]{1,0:T(1,128)} %keep_hbm.1, bf16[2,768,3072]{2,1,0:T(8,128)(2,1)} %wi_hbm.1, bf16[2,3072,768]{2,1,0:T(8,128)(2,1)} %wo_hbm.1), custom_call_target="tpu_custom_call" | custom-call | tf_op jit(solution)/shard_map/moe_layer/pallas_call | solution.py:216
  91.8 2.7 %copy.8 = bf16[1,1024,768]{2,1,0:T(8,128)(2,1)} copy(bf16[1,1024,768]{2,1,0:T(8,128)(2,1)} %bitcast.6) | data formatting | bytes 3145728

commit v2 on v1

--- a/solution.py
+++ b/solution.py
@@ -14,15 +14,14 @@
 CHUNK = 8
 
 
-def step_offsets(side):
-    hop = lambda d: min(d, side - d)
-    chips = [(dy, dx) for dy in range(side) for dx in range(side)]
-    kinds = [(2, 1), (1, 1), (2, 2), (2, 0), (0, 0), (1, 0)]
-    order = []
-    for kind in kinds:
-        same = [c for c in chips if tuple(sorted((hop(c[0]), hop(c[1])), reverse=True)) == kind]
-        order += [(dy, dx, core) for core in range(2) for (dy, dx) in same]
-    return order
+def step_offsets():
+    knights = [[(2, 1), (1, 2), (0, -1), (-1, 0)], [(2, -1), (-1, 2), (0, 1), (1, 0)]]
+    corners = [(1, 1), (-1, -1), (1, -1), (-1, 1)]
+    across = [(0, 2), (2, 0), (2, 2)]
+    order = [(y, x, core) for core in range(2) for half in knights for (y, x) in half]
+    order += [(y, x, core) for core in range(2) for (y, x) in corners]
+    order += [(y, x, core) for core in range(2) for (y, x) in across]
+    return order + [(0, 0, 1), (0, 0, 0)]
 
 
 def layer_kernel(
@@ -52,8 +51,7 @@
 
     barrier = pltpu.get_barrier_semaphore()
 
-    @pl.loop(0, n)
-    def _(k):
+    for k in range(n):
         pl.semaphore_signal(barrier, inc=1, device_id={"ep": k}, device_id_type=MESH)
 
     me = lax.axis_index("ep")
@@ -178,19 +176,21 @@
                 home_copy[k].start()
 
     block = 256
-    for c in range(chunks):
-        for k in range(c * CHUNK, (c + 1) * CHUNK):
+    pieces = [(c * CHUNK, (c + 1) * CHUNK) for c in range(chunks - 1)]
+    pieces += [(steps - CHUNK, steps - CHUNK // 2), (steps - CHUNK // 2, steps)]
+    for lo, hi in pieces:
+        for k in range(lo, hi):
             if k != self_step:
                 home_copy[k].wait_recv()
 
         @pl.loop(0, token_count // block)
         def _(i):
             r = pl.ds(pl.multiple_of(i * block, block), block)
-            y = home[c * CHUNK:(c + 1) * CHUNK].reshape(span, model_dim)
-            part = jnp.dot(cw[r, c * span:(c + 1) * span], y, preferred_element_type=F32)
-            if c > 0:
+            y = home[lo:hi].reshape((hi - lo) * rows, model_dim)
+            part = jnp.dot(cw[r, lo * rows:hi * rows], y, preferred_element_type=F32)
+            if lo > 0:
                 part = acc[r, :] + part
-            if c < chunks - 1:
+            if hi < steps:
                 acc[r, :] = part
             else:
                 out_ref[r, :] = part.astype(BF16)
@@ -203,7 +203,7 @@
 
 def solution(mesh):
     n = mesh.shape["ep"]
-    offsets = step_offsets(math.isqrt(n // 2))
+    offsets = step_offsets()
 
     def local_layer(tokens, w_gate, expert_ids, keep_second, w_in, w_out):
         token_count, model_dim = tokens.shape[1:]
@@ -211,7 +211,7 @@
         local_experts, _, hidden_dim = w_in.shape
         capacity = 2 * token_count // expert_count
         rows = local_experts * capacity
-        any_space = pl.BlockSpec(memory_space=pl.ANY)
+        any_space = pl.BlockSpec(memory_space=pltpu.HBM)
         vmem = pltpu.VMEM
         out = pl.pallas_call(
             functools.partial(layer_kernel, n, offsets),
@@ -240,9 +240,10 @@
                 pltpu.SemaphoreType.DMA((n,)),
             ],
             compiler_params=pltpu.CompilerParams(
-                collective_id=0, has_side_effects=True, vmem_limit_bytes=60 * 1024 * 1024),
+                collective_id=0, has_side_effects=True, vmem_limit_bytes=48 * 1024 * 1024),
             name="moe_layer",
-        )(tokens[0], w_gate.T, expert_ids[0].T, keep_second, w_in, w_out)
+        )(*[pltpu.with_memory_space_constraint(x, pltpu.HBM)
+            for x in (tokens[0], w_gate.T, expert_ids[0].T, keep_second, w_in, w_out)])
         return out[None]
 
     group_spec = P(("dp", "ep"))

time: 94.5 us -> 89.3 us (0.945)
  Pallas kernels: 91.8 us -> 87.9 us
  local copies, waits for them, and re-layouts: 2.65 us -> 1.15 us
    pallas_call x1, Pallas kernels: 91.8 us -> 87.9 us  [local_layer(): pl.pallas_call(functools.partial(layer_kernel, n, offsets), out_shape=jax...]
    unnamed x1, local copies, waits for them, and re-layouts: 2.65 us -> 1.15 us
where the time goes in v2:
time: 89.3 us; the launch traced here: 89 us
  Pallas kernels  87.9 us (98%)
  local copies, waits for them, and re-layouts  1.15 us (1%)
    pallas_call x1, Pallas kernels, local_layer(): pl.pallas_call(functools.partial(layer_kernel, n, offsets), out_shape=jax...  87.9 us

profile of v2, /device:TPU:97, one launch (start us, length us, event | category | flops | bytes accessed | tf_op | source)
XLA Modules:
  0.0 89.0 jit_solution(12915522076865995380)
XLA Ops:
  0.0 87.9 %moe_layer.1 = bf16[1024,768]{1,0:T(8,128)(2,1)S(1)} custom-call(bf16[1024,768]{1,0:T(8,128)(2,1)} %bitcast.7, bf16[64,768]{1,0:T(8,128)(2,1)} %bitcast.8, s32[2,1024]{1,0:T(2,128)} %bitcast.9, s32[1,1024]{1,0:T(1,128)} %keep_hbm.1, bf16[2,768,3072]{2,1,0:T(8,128)(2,1)} %wi_hbm.1, bf16[2,3072,768]{2,1,0:T(8,128)(2,1)} %wo_hbm.1), custom_call_target="tpu_custom_call" | custom-call | tf_op jit(solution)/shard_map/moe_layer/pallas_call | solution.py:216
  87.9 1.1 %copy.8 = bf16[1,1024,768]{2,1,0:T(8,128)(2,1)} copy(bf16[1,1024,768]{2,1,0:T(8,128)(2,1)S(1)} %bitcast.6) | data formatting | bytes 3145728

commit v3 on v2

--- a/solution.py
+++ b/solution.py
@@ -15,12 +15,13 @@
 
 
 def step_offsets():
-    knights = [[(2, 1), (1, 2), (0, -1), (-1, 0)], [(2, -1), (-1, 2), (0, 1), (1, 0)]]
-    corners = [(1, 1), (-1, -1), (1, -1), (-1, 1)]
-    across = [(0, 2), (2, 0), (2, 2)]
-    order = [(y, x, core) for core in range(2) for half in knights for (y, x) in half]
-    order += [(y, x, core) for core in range(2) for (y, x) in corners]
-    order += [(y, x, core) for core in range(2) for (y, x) in across]
+    chunks = [
+        [(2, 1), (2, -1), (0, 1), (0, -1)],
+        [(1, 2), (-1, 2), (1, 0), (-1, 0)],
+        [(1, 1), (-1, -1), (1, -1), (-1, 1)],
+        [(0, 2), (2, 0), (2, 2)],
+    ]
+    order = [(y, x, core) for chunk in chunks for core in range(2) for (y, x) in chunk]
     return order + [(0, 0, 1), (0, 0, 0)]
 
 
@@ -41,18 +42,11 @@
 
     loads = [
         pltpu.make_async_copy(src, dst, local_sem.at[i])
-        for i, (src, dst) in enumerate([(ids_hbm, ids), (keep_hbm, keep), (tok_hbm, tok), (wg_hbm, wg)])
+        for i, (src, dst) in enumerate(
+            [(ids_hbm, ids), (keep_hbm, keep), (tok_hbm, tok), (wg_hbm, wg), (wi_hbm, wi), (wo_hbm, wo)])
     ]
-    for e in range(local_experts):
-        loads.append(pltpu.make_async_copy(wi_hbm.at[e], wi.at[e], local_sem.at[4 + 2 * e]))
-        loads.append(pltpu.make_async_copy(wo_hbm.at[e], wo.at[e], local_sem.at[5 + 2 * e]))
     for load in loads[:4]:
         load.start()
-
-    barrier = pltpu.get_barrier_semaphore()
-
-    for k in range(n):
-        pl.semaphore_signal(barrier, inc=1, device_id={"ep": k}, device_id_type=MESH)
 
     me = lax.axis_index("ep")
     my_y, my_x, my_core = me // (2 * side), (me // 2) % side, me % 2
@@ -65,13 +59,33 @@
     dst = [peer(k, 1) for k in range(steps)]
     src = [peer(k, -1) for k in range(steps)]
 
-    def remote(buf_from, buf_to, ssem, rsem, k, device):
+    hop = lambda d: min(d % side, -d % side)
+    barrier = pltpu.get_barrier_semaphore()
+    for k in sorted(range(steps - 1), key=lambda k: -hop(offsets[k][0]) - hop(offsets[k][1])):
+        pl.semaphore_signal(barrier, inc=1, device_id={"ep": dst[k]}, device_id_type=MESH)
+
+    forth_runs = [(c * CHUNK, min((c + 1) * CHUNK, steps - 1)) for c in range(chunks)]
+    home_runs = forth_runs[:-1] + [(steps - CHUNK, steps - CHUNK // 2), (steps - CHUNK // 2, steps - 1)]
+
+    def remote(buf_from, buf_to, ssem, rsem, lo, hi, run, device):
         return pltpu.make_async_remote_copy(
-            src_ref=buf_from.at[k], dst_ref=buf_to.at[k], send_sem=ssem.at[k], recv_sem=rsem.at[k],
+            src_ref=buf_from.at[lo:hi], dst_ref=buf_to.at[lo:hi], send_sem=ssem.at[0], recv_sem=rsem.at[run],
             device_id={"ep": device}, device_id_type=MESH)
 
-    forth = [remote(send, recv, fs_sem, fr_sem, k, dst[k]) for k in range(steps)]
-    home_copy = [remote(back, home, bs_sem, br_sem, k, src[k]) for k in range(steps)]
+    def run_of(runs, k):
+        return next(i for i, (lo, hi) in enumerate(runs) if lo <= k < hi)
+
+    def start_forth(k):
+        remote(send, recv, fs_sem, fr_sem, k, k + 1, run_of(forth_runs, k), dst[k]).start()
+
+    def start_home(k):
+        remote(back, home, bs_sem, br_sem, k, k + 1, run_of(home_runs, k), src[k]).start()
+
+    def wait_forth(run):
+        remote(send, recv, fs_sem, fr_sem, *forth_runs[run], run, me).wait_recv()
+
+    def wait_home(run):
+        remote(back, home, bs_sem, br_sem, *home_runs[run], run, me).wait_recv()
 
     loads[0].wait()
     loads[1].wait()
@@ -101,23 +115,22 @@
     slot_second = jnp.where(used & (pos_second < capacity), second_id * capacity + pos_second, -1)
 
     loads[2].wait()
-    for c in range(chunks):
-        for j in range(CHUNK):
-            slot = dst[c * CHUNK + j] * rows + lax.broadcasted_iota(jnp.int32, (rows, token_count), 0)
+    for lo, hi in [(0, CHUNK // 2), (CHUNK // 2, CHUNK)] + [(c * CHUNK, (c + 1) * CHUNK) for c in range(1, chunks)]:
+        for k in range(lo, hi):
+            slot = dst[k] * rows + lax.broadcasted_iota(jnp.int32, (rows, token_count), 0)
             hit = (slot == slot_first) | (slot == slot_second)
-            onehot[j * rows:(j + 1) * rows, :] = jnp.where(hit, 1.0, 0.0).astype(BF16)
+            onehot[(k - lo) * rows:(k - lo + 1) * rows, :] = jnp.where(hit, 1.0, 0.0).astype(BF16)
         for col in range(0, model_dim, width):
-            picked = jnp.dot(onehot[...], tok[:, col:col + width], preferred_element_type=F32).astype(BF16)
-            for j in range(CHUNK):
-                k = c * CHUNK + j
+            picked = jnp.dot(onehot[:(hi - lo) * rows, :], tok[:, col:col + width], preferred_element_type=F32).astype(BF16)
+            for k in range(lo, hi):
                 target = recv if k == self_step else send
-                target[k, :, col:col + width] = picked[j * rows:(j + 1) * rows]
-        if c == 0:
-            pl.semaphore_wait(barrier, n)
-        for k in range(c * CHUNK, (c + 1) * CHUNK):
+                target[k, :, col:col + width] = picked[(k - lo) * rows:(k - lo + 1) * rows]
+        if lo == 0:
+            pl.semaphore_wait(barrier, n - 1)
+        for k in range(lo, hi):
             if k != self_step:
-                forth[k].start()
-        if c == 0:
+                start_forth(k)
+        if lo == 0:
             for load in loads[4:]:
                 load.start()
 
@@ -152,9 +165,7 @@
     for load in loads[4:]:
         load.wait()
     for c in range(chunks):
-        for k in range(c * CHUNK, (c + 1) * CHUNK):
-            if k != self_step:
-                forth[k].wait_recv()
+        wait_forth(c)
 
         @pl.loop(0, local_experts)
         def _(e):
@@ -173,15 +184,12 @@
 
         for k in range(c * CHUNK, (c + 1) * CHUNK):
             if k != self_step:
-                home_copy[k].start()
+                start_home(k)
 
     block = 256
-    pieces = [(c * CHUNK, (c + 1) * CHUNK) for c in range(chunks - 1)]
-    pieces += [(steps - CHUNK, steps - CHUNK // 2), (steps - CHUNK // 2, steps)]
-    for lo, hi in pieces:
-        for k in range(lo, hi):
-            if k != self_step:
-                home_copy[k].wait_recv()
+    for run, (lo, hi) in enumerate(home_runs):
+        wait_home(run)
+        hi = steps if hi == steps - 1 else hi
 
         @pl.loop(0, token_count // block)
         def _(i):
@@ -195,10 +203,8 @@
             else:
                 out_ref[r, :] = part.astype(BF16)
 
-    for k in range(steps):
-        if k != self_step:
-            forth[k].wait_send()
-            home_copy[k].wait_send()
+    remote(send, recv, fs_sem, fr_sem, 0, steps - 1, 0, me).wait_send()
+    remote(back, home, bs_sem, br_sem, 0, steps - 1, 0, me).wait_send()
 
 
 def solution(mesh):
@@ -233,11 +239,11 @@
                 vmem((token_count, 128), F32),
                 vmem((token_count, n * rows), BF16),
                 vmem((token_count, model_dim), F32),
-                pltpu.SemaphoreType.DMA((4 + 2 * local_experts,)),
-                pltpu.SemaphoreType.DMA((n,)),
-                pltpu.SemaphoreType.DMA((n,)),
-                pltpu.SemaphoreType.DMA((n,)),
-                pltpu.SemaphoreType.DMA((n,)),
+                pltpu.SemaphoreType.DMA((6,)),
+                pltpu.SemaphoreType.DMA((1,)),
+                pltpu.SemaphoreType.DMA((n // CHUNK,)),
+                pltpu.SemaphoreType.DMA((1,)),
+                pltpu.SemaphoreType.DMA((n // CHUNK + 1,)),
             ],
             compiler_params=pltpu.CompilerParams(
                 collective_id=0, has_side_effects=True, vmem_limit_bytes=48 * 1024 * 1024),

time: 89.3 us -> 86.9 us (0.973)
  Pallas kernels: 87.9 us -> 85.6 us
    pallas_call x1, Pallas kernels: 87.9 us -> 85.6 us  [local_layer(): pl.pallas_call(functools.partial(layer_kernel, n, offsets), out_shape=jax...]
where the time goes in v3:
time: 86.9 us; the launch traced here: 86.8 us
  Pallas kernels  85.6 us (99%)
  local copies, waits for them, and re-layouts  1.15 us (1%)
    pallas_call x1, Pallas kernels, local_layer(): pl.pallas_call(functools.partial(layer_kernel, n, offsets), out_shape=jax...  85.6 us

profile of v3, /device:TPU:97, one launch (start us, length us, event | category | flops | bytes accessed | tf_op | source)
XLA Modules:
  0.0 86.8 jit_solution(4019362939374621062)
XLA Ops:
  0.0 85.6 %moe_layer.1 = bf16[1024,768]{1,0:T(8,128)(2,1)S(1)} custom-call(bf16[1024,768]{1,0:T(8,128)(2,1)} %bitcast.7, bf16[64,768]{1,0:T(8,128)(2,1)} %bitcast.8, s32[2,1024]{1,0:T(2,128)} %bitcast.9, s32[1,1024]{1,0:T(1,128)} %keep_hbm.1, bf16[2,768,3072]{2,1,0:T(8,128)(2,1)} %wi_hbm.1, bf16[2,3072,768]{2,1,0:T(8,128)(2,1)} %wo_hbm.1), custom_call_target="tpu_custom_call" | custom-call | tf_op jit(solution)/shard_map/moe_layer/pallas_call | solution.py:222
  85.6 1.1 %copy.8 = bf16[1,1024,768]{2,1,0:T(8,128)(2,1)} copy(bf16[1,1024,768]{2,1,0:T(8,128)(2,1)S(1)} %bitcast.6) | data formatting | bytes 3145728

commit v4 on v3

--- a/solution.py
+++ b/solution.py
@@ -18,11 +18,15 @@
     chunks = [
         [(2, 1), (2, -1), (0, 1), (0, -1)],
         [(1, 2), (-1, 2), (1, 0), (-1, 0)],
+        [(0, 2), (2, 0), (2, 2)],
         [(1, 1), (-1, -1), (1, -1), (-1, 1)],
-        [(0, 2), (2, 0), (2, 2)],
     ]
-    order = [(y, x, core) for chunk in chunks for core in range(2) for (y, x) in chunk]
-    return order + [(0, 0, 1), (0, 0, 0)]
+    order = []
+    for chunk in chunks:
+        order += [(y, x, core) for core in range(2) for (y, x) in chunk]
+        if len(chunk) < CHUNK // 2:
+            order += [(0, 0, 1), (0, 0, 0)]
+    return order
 
 
 def layer_kernel(
@@ -61,11 +65,15 @@
 
     hop = lambda d: min(d % side, -d % side)
     barrier = pltpu.get_barrier_semaphore()
-    for k in sorted(range(steps - 1), key=lambda k: -hop(offsets[k][0]) - hop(offsets[k][1])):
+    peers = [k for k in range(steps) if k != self_step]
+    for k in sorted(peers, key=lambda k: -hop(offsets[k][0]) - hop(offsets[k][1])):
         pl.semaphore_signal(barrier, inc=1, device_id={"ep": dst[k]}, device_id_type=MESH)
 
-    forth_runs = [(c * CHUNK, min((c + 1) * CHUNK, steps - 1)) for c in range(chunks)]
-    home_runs = forth_runs[:-1] + [(steps - CHUNK, steps - CHUNK // 2), (steps - CHUNK // 2, steps - 1)]
+    forth_runs = [(c * CHUNK, (c + 1) * CHUNK) for c in range(chunks)]
+    home_runs = forth_runs[:-1] + [(steps - CHUNK, steps - CHUNK // 2), (steps - CHUNK // 2, steps)]
+
+    def travel(lo, hi):
+        return lo, hi - 1 if hi - 1 == self_step else hi
 
     def remote(buf_from, buf_to, ssem, rsem, lo, hi, run, device):
         return pltpu.make_async_remote_copy(
@@ -82,10 +90,10 @@
         remote(back, home, bs_sem, br_sem, k, k + 1, run_of(home_runs, k), src[k]).start()
 
     def wait_forth(run):
-        remote(send, recv, fs_sem, fr_sem, *forth_runs[run], run, me).wait_recv()
+        remote(send, recv, fs_sem, fr_sem, *travel(*forth_runs[run]), run, me).wait_recv()
 
     def wait_home(run):
-        remote(back, home, bs_sem, br_sem, *home_runs[run], run, me).wait_recv()
+        remote(back, home, bs_sem, br_sem, *travel(*home_runs[run]), run, me).wait_recv()
 
     loads[0].wait()
     loads[1].wait()
@@ -189,7 +197,6 @@
     block = 256
     for run, (lo, hi) in enumerate(home_runs):
         wait_home(run)
-        hi = steps if hi == steps - 1 else hi
 
         @pl.loop(0, token_count // block)
         def _(i):
@@ -203,8 +210,10 @@
             else:
                 out_ref[r, :] = part.astype(BF16)
 
-    remote(send, recv, fs_sem, fr_sem, 0, steps - 1, 0, me).wait_send()
-    remote(back, home, bs_sem, br_sem, 0, steps - 1, 0, me).wait_send()
+    for lo, hi in ((0, self_step), (self_step + 1, steps)):
+        if lo < hi:
+            remote(send, recv, fs_sem, fr_sem, lo, hi, 0, me).wait_send()
+            remote(back, home, bs_sem, br_sem, lo, hi, 0, me).wait_send()
 
 
 def solution(mesh):

time: 86.9 us -> 87.3 us (level)
  no operation moved by 1% of the time
where the time goes in v4:
time: 87.3 us; the launch traced here: 87.2 us
  Pallas kernels  86 us (99%)
  local copies, waits for them, and re-layouts  1.15 us (1%)
    pallas_call x1, Pallas kernels, local_layer(): pl.pallas_call(functools.partial(layer_kernel, n, offsets), out_shape=jax...  86 us

profile of v4, /device:TPU:97, one launch (start us, length us, event | category | flops | bytes accessed | tf_op | source)
XLA Modules:
  0.0 87.2 jit_solution(10438253162813212581)
XLA Ops:
  0.0 86.0 %moe_layer.1 = bf16[1024,768]{1,0:T(8,128)(2,1)S(1)} custom-call(bf16[1024,768]{1,0:T(8,128)(2,1)} %bitcast.7, bf16[64,768]{1,0:T(8,128)(2,1)} %bitcast.8, s32[2,1024]{1,0:T(2,128)} %bitcast.9, s32[1,1024]{1,0:T(1,128)} %keep_hbm.1, bf16[2,768,3072]{2,1,0:T(8,128)(2,1)} %wi_hbm.1, bf16[2,3072,768]{2,1,0:T(8,128)(2,1)} %wo_hbm.1), custom_call_target="tpu_custom_call" | custom-call | tf_op jit(solution)/shard_map/moe_layer/pallas_call | solution.py:231
  86.0 1.1 %copy.8 = bf16[1,1024,768]{2,1,0:T(8,128)(2,1)} copy(bf16[1,1024,768]{2,1,0:T(8,128)(2,1)S(1)} %bitcast.6) | data formatting | bytes 3145728

commit v5 on v4

--- a/solution.py
+++ b/solution.py
@@ -16,10 +16,10 @@
 
 def step_offsets():
     chunks = [
+        [(1, 1), (-1, -1), (1, -1), (-1, 1)],
         [(2, 1), (2, -1), (0, 1), (0, -1)],
         [(1, 2), (-1, 2), (1, 0), (-1, 0)],
         [(0, 2), (2, 0), (2, 2)],
-        [(1, 1), (-1, -1), (1, -1), (-1, 1)],
     ]
     order = []
     for chunk in chunks:
@@ -32,7 +32,7 @@
 def layer_kernel(
     n, offsets, tok_hbm, wg_hbm, ids_hbm, keep_hbm, wi_hbm, wo_hbm, out_ref,
     tok, wg, ids, keep, wi, wo, onehot, send, recv, back, home, cols, cw, acc,
-    local_sem, fs_sem, fr_sem, bs_sem, br_sem,
+    ready_sem, local_sem, fs_sem, fr_sem, bs_sem, br_sem,
 ):
     side = math.isqrt(n // 2)
     token_count, model_dim = tok.shape
@@ -64,9 +64,11 @@
     src = [peer(k, -1) for k in range(steps)]
 
     hop = lambda d: min(d % side, -d % side)
+    peers = [k for k in range(steps) if k != self_step]
+    near = [k for k in peers if hop(offsets[k][0]) + hop(offsets[k][1]) <= 2]
+    assert all(k in near for k in range(CHUNK))
     barrier = pltpu.get_barrier_semaphore()
-    peers = [k for k in range(steps) if k != self_step]
-    for k in sorted(peers, key=lambda k: -hop(offsets[k][0]) - hop(offsets[k][1])):
+    for k in sorted(near, key=lambda k: -hop(offsets[k][0]) - hop(offsets[k][1])):
         pl.semaphore_signal(barrier, inc=1, device_id={"ep": dst[k]}, device_id_type=MESH)
 
     forth_runs = [(c * CHUNK, (c + 1) * CHUNK) for c in range(chunks)]
@@ -122,6 +124,10 @@
     slot_first = jnp.where(pos_first < capacity, first_id * capacity + pos_first, -1)
     slot_second = jnp.where(used & (pos_second < capacity), second_id * capacity + pos_second, -1)
 
+    pl.semaphore_wait(barrier, len(near))
+    for k in near:
+        pl.semaphore_signal(ready_sem, inc=1, device_id={"ep": dst[k]}, device_id_type=MESH)
+
     loads[2].wait()
     for lo, hi in [(0, CHUNK // 2), (CHUNK // 2, CHUNK)] + [(c * CHUNK, (c + 1) * CHUNK) for c in range(1, chunks)]:
         for k in range(lo, hi):
@@ -133,8 +139,8 @@
             for k in range(lo, hi):
                 target = recv if k == self_step else send
                 target[k, :, col:col + width] = picked[(k - lo) * rows:(k - lo + 1) * rows]
-        if lo == 0:
-            pl.semaphore_wait(barrier, n - 1)
+        if lo == CHUNK:
+            pl.semaphore_wait(ready_sem, len(near))
         for k in range(lo, hi):
             if k != self_step:
                 start_forth(k)
@@ -248,6 +254,7 @@
                 vmem((token_count, 128), F32),
                 vmem((token_count, n * rows), BF16),
                 vmem((token_count, model_dim), F32),
+                pltpu.SemaphoreType.REGULAR,
                 pltpu.SemaphoreType.DMA((6,)),
                 pltpu.SemaphoreType.DMA((1,)),
                 pltpu.SemaphoreType.DMA((n // CHUNK,)),

time: 87.3 us -> 89.5 us (1.025)
  the two profiles are of different devices: /device:TPU:97 before, /device:TPU:104 now
where the time goes in v5:
time: 89.5 us; the launch traced here: 89.3 us
  Pallas kernels  88.2 us (99%)
  local copies, waits for them, and re-layouts  1.15 us (1%)
    pallas_call x1, Pallas kernels, local_layer(): pl.pallas_call(functools.partial(layer_kernel, n, offsets), out_shape=jax...  88.2 us

profile of v5, /device:TPU:104, one launch (start us, length us, event | category | flops | bytes accessed | tf_op | source)
XLA Modules:
  0.0 89.3 jit_solution(16064608480074724447)
XLA Ops:
  0.0 88.2 %moe_layer.1 = bf16[1024,768]{1,0:T(8,128)(2,1)S(1)} custom-call(bf16[1024,768]{1,0:T(8,128)(2,1)} %bitcast.7, bf16[64,768]{1,0:T(8,128)(2,1)} %bitcast.8, s32[2,1024]{1,0:T(2,128)} %bitcast.9, s32[1,1024]{1,0:T(1,128)} %keep_hbm.1, bf16[2,768,3072]{2,1,0:T(8,128)(2,1)} %wi_hbm.1, bf16[2,3072,768]{2,1,0:T(8,128)(2,1)} %wo_hbm.1), custom_call_target="tpu_custom_call" | custom-call | tf_op jit(solution)/shard_map/moe_layer/pallas_call | solution.py:237
  88.2 1.1 %copy.8 = bf16[1,1024,768]{2,1,0:T(8,128)(2,1)} copy(bf16[1,1024,768]{2,1,0:T(8,128)(2,1)S(1)} %bitcast.6) | data formatting | bytes 3145728

commit v6 on v5

--- a/solution.py
+++ b/solution.py
@@ -16,10 +16,10 @@
 
 def step_offsets():
     chunks = [
+        [(0, 1), (0, -1), (1, 0), (-1, 0)],
         [(1, 1), (-1, -1), (1, -1), (-1, 1)],
-        [(2, 1), (2, -1), (0, 1), (0, -1)],
-        [(1, 2), (-1, 2), (1, 0), (-1, 0)],
         [(0, 2), (2, 0), (2, 2)],
+        [(2, 1), (1, 2), (2, -1), (-1, 2)],
     ]
     order = []
     for chunk in chunks:

time: 89.5 us -> 87.4 us (0.977)
  the two profiles are of different devices: /device:TPU:104 before, /device:TPU:97 now
where the time goes in v6:
time: 87.4 us; the launch traced here: 87.2 us
  Pallas kernels  86.1 us (99%)
  local copies, waits for them, and re-layouts  1.15 us (1%)
    pallas_call x1, Pallas kernels, local_layer(): pl.pallas_call(functools.partial(layer_kernel, n, offsets), out_shape=jax...  86.1 us

profile of v6, /device:TPU:97, one launch (start us, length us, event | category | flops | bytes accessed | tf_op | source)
XLA Modules:
  0.0 87.2 jit_solution(10296445681349299304)
XLA Ops:
  0.0 86.1 %moe_layer.1 = bf16[1024,768]{1,0:T(8,128)(2,1)S(1)} custom-call(bf16[1024,768]{1,0:T(8,128)(2,1)} %bitcast.7, bf16[64,768]{1,0:T(8,128)(2,1)} %bitcast.8, s32[2,1024]{1,0:T(2,128)} %bitcast.9, s32[1,1024]{1,0:T(1,128)} %keep_hbm.1, bf16[2,768,3072]{2,1,0:T(8,128)(2,1)} %wi_hbm.1, bf16[2,3072,768]{2,1,0:T(8,128)(2,1)} %wo_hbm.1), custom_call_target="tpu_custom_call" | custom-call | tf_op jit(solution)/shard_map/moe_layer/pallas_call | solution.py:237
  86.1 1.1 %copy.8 = bf16[1,1024,768]{2,1,0:T(8,128)(2,1)} copy(bf16[1,1024,768]{2,1,0:T(8,128)(2,1)S(1)} %bitcast.6) | data formatting | bytes 3145728

commit v7 on v4

--- a/solution.py
+++ b/solution.py
@@ -18,8 +18,8 @@
     chunks = [
         [(2, 1), (2, -1), (0, 1), (0, -1)],
         [(1, 2), (-1, 2), (1, 0), (-1, 0)],
+        [(1, 1), (-1, -1), (1, -1), (-1, 1)],
         [(0, 2), (2, 0), (2, 2)],
-        [(1, 1), (-1, -1), (1, -1), (-1, 1)],
     ]
     order = []
     for chunk in chunks:
@@ -30,9 +30,9 @@
 
 
 def layer_kernel(
-    n, offsets, tok_hbm, wg_hbm, ids_hbm, keep_hbm, wi_hbm, wo_hbm, out_ref,
-    tok, wg, ids, keep, wi, wo, onehot, send, recv, back, home, cols, cw, acc,
-    local_sem, fs_sem, fr_sem, bs_sem, br_sem,
+    n, offsets, tok_hbm, wg_hbm, ids_hbm, keep_hbm, wi_hbm, wo_hbm, acc, last_cw, last_home,
+    tok, wg, ids, keep, wi, wo, onehot, send, recv, back, home, cols, cw,
+    ready_sem, local_sem, fs_sem, fr_sem, bs_sem, br_sem,
 ):
     side = math.isqrt(n // 2)
     token_count, model_dim = tok.shape
@@ -63,10 +63,11 @@
     dst = [peer(k, 1) for k in range(steps)]
     src = [peer(k, -1) for k in range(steps)]
 
-    hop = lambda d: min(d % side, -d % side)
+    hops = [sum(min(d % side, -d % side) for d in (y, x)) for (y, x, _) in offsets]
+    near = sorted((k for k in range(steps) if k != self_step and hops[k] <= 3), key=lambda k: -hops[k])
+    first_far = min(k for k in range(steps) if hops[k] > 3) // CHUNK * CHUNK
     barrier = pltpu.get_barrier_semaphore()
-    peers = [k for k in range(steps) if k != self_step]
-    for k in sorted(peers, key=lambda k: -hop(offsets[k][0]) - hop(offsets[k][1])):
+    for k in near:
         pl.semaphore_signal(barrier, inc=1, device_id={"ep": dst[k]}, device_id_type=MESH)
 
     forth_runs = [(c * CHUNK, (c + 1) * CHUNK) for c in range(chunks)]
@@ -134,11 +135,15 @@
                 target = recv if k == self_step else send
                 target[k, :, col:col + width] = picked[(k - lo) * rows:(k - lo + 1) * rows]
         if lo == 0:
-            pl.semaphore_wait(barrier, n - 1)
+            pl.semaphore_wait(barrier, len(near))
+        if lo == first_far:
+            pl.semaphore_wait(ready_sem, len(near))
         for k in range(lo, hi):
             if k != self_step:
                 start_forth(k)
         if lo == 0:
+            for k in near:
+                pl.semaphore_signal(ready_sem, inc=1, device_id={"ep": dst[k]}, device_id_type=MESH)
             for load in loads[4:]:
                 load.start()
 
@@ -168,7 +173,10 @@
             r = pl.ds(pl.multiple_of(i * block, block), block)
             line = cols[r, :]
             weight = jnp.where(line[:, 0:1] == slot, line[:, 2:3], 0.0) + jnp.where(line[:, 1:2] == slot, line[:, 3:4], 0.0)
-            cw[r, c * span:(c + 1) * span] = weight.astype(BF16)
+            weight = weight.astype(BF16)
+            cw[r, c * span:(c + 1) * span] = weight
+            if c == chunks - 1:
+                last_cw[r, :] = weight[:, span // 2:]
 
     for load in loads[4:]:
         load.wait()
@@ -195,7 +203,7 @@
                 start_home(k)
 
     block = 256
-    for run, (lo, hi) in enumerate(home_runs):
+    for run, (lo, hi) in enumerate(home_runs[:-1]):
         wait_home(run)
 
         @pl.loop(0, token_count // block)
@@ -205,15 +213,28 @@
             part = jnp.dot(cw[r, lo * rows:hi * rows], y, preferred_element_type=F32)
             if lo > 0:
                 part = acc[r, :] + part
-            if hi < steps:
-                acc[r, :] = part
-            else:
-                out_ref[r, :] = part.astype(BF16)
-
+            acc[r, :] = part
+
+    lo, hi = home_runs[-1]
+    wait_home(len(home_runs) - 1)
+    last_home[...] = home[lo:hi].reshape((hi - lo) * rows, model_dim)
     for lo, hi in ((0, self_step), (self_step + 1, steps)):
         if lo < hi:
             remote(send, recv, fs_sem, fr_sem, lo, hi, 0, me).wait_send()
             remote(back, home, bs_sem, br_sem, lo, hi, 0, me).wait_send()
+
+
+def finish_kernel(acc, last_cw, last_home, out_hbm, out, sem):
+    block = 256
+    copies = []
+    for i in range(out.shape[0] // block):
+        r = pl.ds(i * block, block)
+        part = acc[r, :] + jnp.dot(last_cw[r, :], last_home[...], preferred_element_type=F32)
+        out[r, :] = part.astype(BF16)
+        copies.append(pltpu.make_async_copy(out.at[r], out_hbm.at[r], sem.at[i]))
+        copies[-1].start()
+    for copy in copies:
+        copy.wait()
 
 
 def solution(mesh):
@@ -228,11 +249,16 @@
         rows = local_experts * capacity
         any_space = pl.BlockSpec(memory_space=pltpu.HBM)
         vmem = pltpu.VMEM
-        out = pl.pallas_call(
+        last = CHUNK // 2 * rows
+        parts = pl.pallas_call(
             functools.partial(layer_kernel, n, offsets),
-            out_shape=jax.ShapeDtypeStruct((token_count, model_dim), BF16),
+            out_shape=[
+                jax.ShapeDtypeStruct((token_count, model_dim), F32),
+                jax.ShapeDtypeStruct((token_count, last), BF16),
+                jax.ShapeDtypeStruct((last, model_dim), BF16),
+            ],
             in_specs=[any_space] * 6,
-            out_specs=pl.BlockSpec(memory_space=vmem),
+            out_specs=[pl.BlockSpec(memory_space=vmem)] * 3,
             scratch_shapes=[
                 vmem((token_count, model_dim), BF16),
                 vmem((expert_count, model_dim), BF16),
@@ -247,7 +273,7 @@
                 vmem((n, rows, model_dim), BF16),
                 vmem((token_count, 128), F32),
                 vmem((token_count, n * rows), BF16),
-                vmem((token_count, model_dim), F32),
+                pltpu.SemaphoreType.REGULAR,
                 pltpu.SemaphoreType.DMA((6,)),
                 pltpu.SemaphoreType.DMA((1,)),
                 pltpu.SemaphoreType.DMA((n // CHUNK,)),
@@ -259,6 +285,15 @@
             name="moe_layer",
         )(*[pltpu.with_memory_space_constraint(x, pltpu.HBM)
             for x in (tokens[0], w_gate.T, expert_ids[0].T, keep_second, w_in, w_out)])
+        out = pl.pallas_call(
+            finish_kernel,
+            out_shape=jax.ShapeDtypeStruct((token_count, model_dim), BF16),
+            in_specs=[pl.BlockSpec(memory_space=vmem)] * 3,
+            out_specs=pl.BlockSpec(memory_space=pltpu.HBM),
+            scratch_shapes=[vmem((token_count, model_dim), BF16), pltpu.SemaphoreType.DMA((token_count // 256,))],
+            compiler_params=pltpu.CompilerParams(vmem_limit_bytes=16 * 1024 * 1024),
+            name="finish",
+        )(*parts)
         return out[None]
 
     group_spec = P(("dp", "ep"))

time: 87.3 us -> 90 us (1.031)
  Pallas kernels: 86 us -> 89.7 us
  local copies, waits for them, and re-layouts: 1.15 us -> 0 us
    pallas_call x1 -> x2, Pallas kernels: 86 us -> 89.7 us  [the longest x1 88.2 us: local_layer(): pl.pallas_call(functools.partial(layer_kernel, n, offsets), out_shape=[ja...]
    unnamed x1 -> x0, local copies, waits for them, and re-layouts: 1.15 us -> none
where the time goes in v7:
time: 90 us; the launch traced here: 89.8 us
  Pallas kernels  89.7 us (100%)
    pallas_call x1, Pallas kernels, local_layer(): pl.pallas_call(functools.partial(layer_kernel, n, offsets), out_shape=[ja...  88.2 us

profile of v7, /device:TPU:97, one launch (start us, length us, event | category | flops | bytes accessed | tf_op | source)
XLA Modules:
  0.0 89.8 jit_solution(2448806843905502312)
XLA Ops:
  0.0 88.2 %moe_layer.1 = (f32[1024,768]{1,0:T(8,128)S(1)}, bf16[1024,256]{1,0:T(8,128)(2,1)S(1)}, bf16[256,768]{1,0:T(8,128)(2,1)S(1)}) custom-call(bf16[1024,768]{1,0:T(8,128)(2,1)} %bitcast.6, bf16[64,768]{1,0:T(8,128)(2,1)} %bitcast.7, s32[2,1024]{1,0:T(2,128)} %bitcast.8, s32[1,1024]{1,0:T(1,128)} %keep_hbm.1, bf16[2,768,3072]{2,1,0:T(8,128)(2,1)} %wi_hbm.1, ...), custom_call_target="tpu_custom_call" | custom-call | tf_op jit(solution)/shard_map/moe_layer/pallas_call | solution.py:253
  88.2 1.5 %finish.1 = bf16[1024,768]{1,0:T(8,128)(2,1)} custom-call(f32[1024,768]{1,0:T(8,128)S(1)} %get-tuple-element.8.acc, bf16[1024,256]{1,0:T(8,128)(2,1)S(1)} %get-tuple-element.9.last_cw, bf16[256,768]{1,0:T(8,128)(2,1)S(1)} %get-tuple-element.10.last_home), custom_call_target="tpu_custom_call" | custom-call | tf_op jit(solution)/shard_map/finish/pallas_call | solution.py:288

commit v8 on v7

--- a/solution.py
+++ b/solution.py
@@ -18,8 +18,8 @@
     chunks = [
         [(2, 1), (2, -1), (0, 1), (0, -1)],
         [(1, 2), (-1, 2), (1, 0), (-1, 0)],
+        [(0, 2), (2, 0), (2, 2)],
         [(1, 1), (-1, -1), (1, -1), (-1, 1)],
-        [(0, 2), (2, 0), (2, 2)],
     ]
     order = []
     for chunk in chunks:
@@ -32,7 +32,7 @@
 def layer_kernel(
     n, offsets, tok_hbm, wg_hbm, ids_hbm, keep_hbm, wi_hbm, wo_hbm, acc, last_cw, last_home,
     tok, wg, ids, keep, wi, wo, onehot, send, recv, back, home, cols, cw,
-    ready_sem, local_sem, fs_sem, fr_sem, bs_sem, br_sem,
+    local_sem, fs_sem, fr_sem, bs_sem, br_sem,
 ):
     side = math.isqrt(n // 2)
     token_count, model_dim = tok.shape
@@ -63,11 +63,10 @@
     dst = [peer(k, 1) for k in range(steps)]
     src = [peer(k, -1) for k in range(steps)]
 
-    hops = [sum(min(d % side, -d % side) for d in (y, x)) for (y, x, _) in offsets]
-    near = sorted((k for k in range(steps) if k != self_step and hops[k] <= 3), key=lambda k: -hops[k])
-    first_far = min(k for k in range(steps) if hops[k] > 3) // CHUNK * CHUNK
+    hop = lambda d: min(d % side, -d % side)
     barrier = pltpu.get_barrier_semaphore()
-    for k in near:
+    peers = [k for k in range(steps) if k != self_step]
+    for k in sorted(peers, key=lambda k: -hop(offsets[k][0]) - hop(offsets[k][1])):
         pl.semaphore_signal(barrier, inc=1, device_id={"ep": dst[k]}, device_id_type=MESH)
 
     forth_runs = [(c * CHUNK, (c + 1) * CHUNK) for c in range(chunks)]
@@ -135,15 +134,11 @@
                 target = recv if k == self_step else send
                 target[k, :, col:col + width] = picked[(k - lo) * rows:(k - lo + 1) * rows]
         if lo == 0:
-            pl.semaphore_wait(barrier, len(near))
-        if lo == first_far:
-            pl.semaphore_wait(ready_sem, len(near))
+            pl.semaphore_wait(barrier, n - 1)
         for k in range(lo, hi):
             if k != self_step:
                 start_forth(k)
         if lo == 0:
-            for k in near:
-                pl.semaphore_signal(ready_sem, inc=1, device_id={"ep": dst[k]}, device_id_type=MESH)
             for load in loads[4:]:
                 load.start()
 
@@ -273,7 +268,6 @@
                 vmem((n, rows, model_dim), BF16),
                 vmem((token_count, 128), F32),
                 vmem((token_count, n * rows), BF16),
-                pltpu.SemaphoreType.REGULAR,
                 pltpu.SemaphoreType.DMA((6,)),
                 pltpu.SemaphoreType.DMA((1,)),
                 pltpu.SemaphoreType.DMA((n // CHUNK,)),

time: 90 us -> 86.7 us (0.963)
  Pallas kernels: 89.7 us -> 86.5 us
    pallas_call x1, Pallas kernels: 88.2 us -> 85 us  [local_layer(): pl.pallas_call(functools.partial(layer_kernel, n, offsets), out_shape=[ja...]
where the time goes in v8:
time: 86.7 us; the launch traced here: 86.6 us
  Pallas kernels  86.5 us (100%)
    pallas_call x1, Pallas kernels, local_layer(): pl.pallas_call(functools.partial(layer_kernel, n, offsets), out_shape=[ja...  85 us

profile of v8, /device:TPU:97, one launch (start us, length us, event | category | flops | bytes accessed | tf_op | source)
XLA Modules:
  0.0 86.6 jit_solution(14198581258062233652)
XLA Ops:
  0.0 85.0 %moe_layer.1 = (f32[1024,768]{1,0:T(8,128)S(1)}, bf16[1024,256]{1,0:T(8,128)(2,1)S(1)}, bf16[256,768]{1,0:T(8,128)(2,1)S(1)}) custom-call(bf16[1024,768]{1,0:T(8,128)(2,1)} %bitcast.6, bf16[64,768]{1,0:T(8,128)(2,1)} %bitcast.7, s32[2,1024]{1,0:T(2,128)} %bitcast.8, s32[1,1024]{1,0:T(1,128)} %keep_hbm.1, bf16[2,768,3072]{2,1,0:T(8,128)(2,1)} %wi_hbm.1, ...), custom_call_target="tpu_custom_call" | custom-call | tf_op jit(solution)/shard_map/moe_layer/pallas_call | solution.py:248
  85.0 1.5 %finish.1 = bf16[1024,768]{1,0:T(8,128)(2,1)} custom-call(f32[1024,768]{1,0:T(8,128)S(1)} %get-tuple-element.8.acc, bf16[1024,256]{1,0:T(8,128)(2,1)S(1)} %get-tuple-element.9.last_cw, bf16[256,768]{1,0:T(8,128)(2,1)S(1)} %get-tuple-element.10.last_home), custom_call_target="tpu_custom_call" | custom-call | tf_op jit(solution)/shard_map/finish/pallas_call | solution.py:282

commit v9 on v7

--- a/solution.py
+++ b/solution.py
@@ -18,8 +18,8 @@
     chunks = [
         [(2, 1), (2, -1), (0, 1), (0, -1)],
         [(1, 2), (-1, 2), (1, 0), (-1, 0)],
+        [(0, 2), (2, 0), (2, 2)],
         [(1, 1), (-1, -1), (1, -1), (-1, 1)],
-        [(0, 2), (2, 0), (2, 2)],
     ]
     order = []
     for chunk in chunks:
@@ -141,9 +141,10 @@
         for k in range(lo, hi):
             if k != self_step:
                 start_forth(k)
-        if lo == 0:
+        if lo == CHUNK // 2:
             for k in near:
                 pl.semaphore_signal(ready_sem, inc=1, device_id={"ep": dst[k]}, device_id_type=MESH)
+        if lo == 0:
             for load in loads[4:]:
                 load.start()
 

time: 90 us -> 84 us (0.933); the launches traced: 89.8 us -> 82.8 us
  Pallas kernels: 89.7 us -> 82.6 us
    pallas_call x1, Pallas kernels: 88.2 us -> 81.2 us  [local_layer(): pl.pallas_call(functools.partial(layer_kernel, n, offsets), out_shape=[ja...]
where the time goes in v9:
time: 84 us; the launch traced here: 82.8 us
  Pallas kernels  82.6 us (98%)
    pallas_call x1, Pallas kernels, local_layer(): pl.pallas_call(functools.partial(layer_kernel, n, offsets), out_shape=[ja...  81.2 us

profile of v9, /device:TPU:97, one launch (start us, length us, event | category | flops | bytes accessed | tf_op | source)
XLA Modules:
  0.0 82.8 jit_solution(14088315002854584596)
XLA Ops:
  0.0 81.2 %moe_layer.1 = (f32[1024,768]{1,0:T(8,128)S(1)}, bf16[1024,256]{1,0:T(8,128)(2,1)S(1)}, bf16[256,768]{1,0:T(8,128)(2,1)S(1)}) custom-call(bf16[1024,768]{1,0:T(8,128)(2,1)} %bitcast.6, bf16[64,768]{1,0:T(8,128)(2,1)} %bitcast.7, s32[2,1024]{1,0:T(2,128)} %bitcast.8, s32[1,1024]{1,0:T(1,128)} %keep_hbm.1, bf16[2,768,3072]{2,1,0:T(8,128)(2,1)} %wi_hbm.1, ...), custom_call_target="tpu_custom_call" | custom-call | tf_op jit(solution)/shard_map/moe_layer/pallas_call | solution.py:254
  81.2 1.5 %finish.1 = bf16[1024,768]{1,0:T(8,128)(2,1)} custom-call(f32[1024,768]{1,0:T(8,128)S(1)} %get-tuple-element.8.acc, bf16[1024,256]{1,0:T(8,128)(2,1)S(1)} %get-tuple-element.9.last_cw, bf16[256,768]{1,0:T(8,128)(2,1)S(1)} %get-tuple-element.10.last_home), custom_call_target="tpu_custom_call" | custom-call | tf_op jit(solution)/shard_map/finish/pallas_call | solution.py:289

commit v10 on v9

--- a/solution.py
+++ b/solution.py
@@ -66,6 +66,7 @@
     hops = [sum(min(d % side, -d % side) for d in (y, x)) for (y, x, _) in offsets]
     near = sorted((k for k in range(steps) if k != self_step and hops[k] <= 3), key=lambda k: -hops[k])
     first_far = min(k for k in range(steps) if hops[k] > 3) // CHUNK * CHUNK
+    halfway = offsets.index((0, side // 2, 0))
     barrier = pltpu.get_barrier_semaphore()
     for k in near:
         pl.semaphore_signal(barrier, inc=1, device_id={"ep": dst[k]}, device_id_type=MESH)
@@ -137,13 +138,12 @@
         if lo == 0:
             pl.semaphore_wait(barrier, len(near))
         if lo == first_far:
-            pl.semaphore_wait(ready_sem, len(near))
+            pl.semaphore_wait(ready_sem, 1)
         for k in range(lo, hi):
             if k != self_step:
                 start_forth(k)
         if lo == CHUNK // 2:
-            for k in near:
-                pl.semaphore_signal(ready_sem, inc=1, device_id={"ep": dst[k]}, device_id_type=MESH)
+            pl.semaphore_signal(ready_sem, inc=1, device_id={"ep": dst[halfway]}, device_id_type=MESH)
         if lo == 0:
             for load in loads[4:]:
                 load.start()

time: 84 us -> 88.5 us (1.054); the launches traced: 82.8 us -> 88.4 us
  Pallas kernels: 82.6 us -> 88.2 us
    pallas_call x1, Pallas kernels: 81.2 us -> 86.8 us  [local_layer(): pl.pallas_call(functools.partial(layer_kernel, n, offsets), out_shape=[ja...]
where the time goes in v10:
time: 88.5 us; the launch traced here: 88.4 us
  Pallas kernels  88.2 us (100%)
    pallas_call x1, Pallas kernels, local_layer(): pl.pallas_call(functools.partial(layer_kernel, n, offsets), out_shape=[ja...  86.8 us

profile of v10, /device:TPU:97, one launch (start us, length us, event | category | flops | bytes accessed | tf_op | source)
XLA Modules:
  0.0 88.4 jit_solution(6826374150529357153)
XLA Ops:
  0.0 86.8 %moe_layer.1 = (f32[1024,768]{1,0:T(8,128)S(1)}, bf16[1024,256]{1,0:T(8,128)(2,1)S(1)}, bf16[256,768]{1,0:T(8,128)(2,1)S(1)}) custom-call(bf16[1024,768]{1,0:T(8,128)(2,1)} %bitcast.6, bf16[64,768]{1,0:T(8,128)(2,1)} %bitcast.7, s32[2,1024]{1,0:T(2,128)} %bitcast.8, s32[1,1024]{1,0:T(1,128)} %keep_hbm.1, bf16[2,768,3072]{2,1,0:T(8,128)(2,1)} %wi_hbm.1, ...), custom_call_target="tpu_custom_call" | custom-call | tf_op jit(solution)/shard_map/moe_layer/pallas_call | solution.py:254
  86.8 1.5 %finish.1 = bf16[1024,768]{1,0:T(8,128)(2,1)} custom-call(f32[1024,768]{1,0:T(8,128)S(1)} %get-tuple-element.8.acc, bf16[1024,256]{1,0:T(8,128)(2,1)S(1)} %get-tuple-element.9.last_cw, bf16[256,768]{1,0:T(8,128)(2,1)S(1)} %get-tuple-element.10.last_home), custom_call_target="tpu_custom_call" | custom-call | tf_op jit(solution)/shard_map/finish/pallas_call | solution.py:289

commit v11 on v9

--- a/solution.py
+++ b/solution.py
@@ -123,8 +123,42 @@
     slot_first = jnp.where(pos_first < capacity, first_id * capacity + pos_first, -1)
     slot_second = jnp.where(used & (pos_second < capacity), second_id * capacity + pos_second, -1)
 
+    def build_weights():
+        loads[3].wait()
+        logits = lax.dot_general(wg[...], tok[...], (((1,), (1,)), ((), ())), preferred_element_type=F32)
+        top = jnp.max(logits, axis=0, keepdims=True)
+        raised = jnp.exp(logits - top)
+        probs = raised / jnp.sum(raised, axis=0, keepdims=True)
+        expert_row = lax.broadcasted_iota(jnp.int32, (expert_count, token_count), 0)
+        gate_first = jnp.sum(jnp.where(expert_row == first_id, probs, 0.0), axis=0, keepdims=True)
+        gate_second = jnp.sum(jnp.where((expert_row == second_id) & used, probs, 0.0), axis=0, keepdims=True)
+        gate_total = gate_first + gate_second
+        lines = jnp.concatenate(
+            [slot_first.astype(F32), slot_second.astype(F32), gate_first / gate_total, gate_second / gate_total,
+             jnp.zeros((124, token_count), F32)], axis=0)
+        cols[...] = jnp.transpose(lines)
+        block = 64
+        for c in range(chunks):
+            lane = lax.broadcasted_iota(jnp.int32, (1, span), 1)
+            slot = lane % rows
+            for j in range(CHUNK):
+                slot = slot + jnp.where(lane // rows == j, dst[c * CHUNK + j] * rows, 0)
+            slot = slot.astype(F32)
+
+            @pl.loop(0, token_count // block)
+            def _(i):
+                r = pl.ds(pl.multiple_of(i * block, block), block)
+                line = cols[r, :]
+                weight = jnp.where(line[:, 0:1] == slot, line[:, 2:3], 0.0) + jnp.where(line[:, 1:2] == slot, line[:, 3:4], 0.0)
+                weight = weight.astype(BF16)
+                cw[r, c * span:(c + 1) * span] = weight
+                if c == chunks - 1:
+                    last_cw[r, :] = weight[:, span // 2:]
+
     loads[2].wait()
     for lo, hi in [(0, CHUNK // 2), (CHUNK // 2, CHUNK)] + [(c * CHUNK, (c + 1) * CHUNK) for c in range(1, chunks)]:
+        if lo == 2 * CHUNK:
+            build_weights()
         for k in range(lo, hi):
             slot = dst[k] * rows + lax.broadcasted_iota(jnp.int32, (rows, token_count), 0)
             hit = (slot == slot_first) | (slot == slot_second)
@@ -147,37 +181,6 @@
         if lo == 0:
             for load in loads[4:]:
                 load.start()
-
-    loads[3].wait()
-    logits = lax.dot_general(wg[...], tok[...], (((1,), (1,)), ((), ())), preferred_element_type=F32)
-    top = jnp.max(logits, axis=0, keepdims=True)
-    raised = jnp.exp(logits - top)
-    probs = raised / jnp.sum(raised, axis=0, keepdims=True)
-    expert_row = lax.broadcasted_iota(jnp.int32, (expert_count, token_count), 0)
-    gate_first = jnp.sum(jnp.where(expert_row == first_id, probs, 0.0), axis=0, keepdims=True)
-    gate_second = jnp.sum(jnp.where((expert_row == second_id) & used, probs, 0.0), axis=0, keepdims=True)
-    gate_total = gate_first + gate_second
-    lines = jnp.concatenate(
-        [slot_first.astype(F32), slot_second.astype(F32), gate_first / gate_total, gate_second / gate_total,
-         jnp.zeros((124, token_count), F32)], axis=0)
-    cols[...] = jnp.transpose(lines)
-    block = 64
-    for c in range(chunks):
-        lane = lax.broadcasted_iota(jnp.int32, (1, span), 1)
-        slot = lane % rows
-        for j in range(CHUNK):
-            slot = slot + jnp.where(lane // rows == j, dst[c * CHUNK + j] * rows, 0)
-        slot = slot.astype(F32)
-
-        @pl.loop(0, token_count // block)
-        def _(i):
-            r = pl.ds(pl.multiple_of(i * block, block), block)
-            line = cols[r, :]
-            weight = jnp.where(line[:, 0:1] == slot, line[:, 2:3], 0.0) + jnp.where(line[:, 1:2] == slot, line[:, 3:4], 0.0)
-            weight = weight.astype(BF16)
-            cw[r, c * span:(c + 1) * span] = weight
-            if c == chunks - 1:
-                last_cw[r, :] = weight[:, span // 2:]
 
     for load in loads[4:]:
         load.wait()

time: 84 us -> 89.2 us (1.062); the launches traced: 82.8 us -> 89 us
  Pallas kernels: 82.6 us -> 88.8 us
    pallas_call x1, Pallas kernels: 81.2 us -> 87.4 us  [local_layer(): pl.pallas_call(functools.partial(layer_kernel, n, offsets), out_shape=[ja...]
where the time goes in v11:
time: 89.2 us; the launch traced here: 89 us
  Pallas kernels  88.8 us (100%)
    pallas_call x1, Pallas kernels, local_layer(): pl.pallas_call(functools.partial(layer_kernel, n, offsets), out_shape=[ja...  87.4 us

profile of v11, /device:TPU:97, one launch (start us, length us, event | category | flops | bytes accessed | tf_op | source)
XLA Modules:
  0.0 89.0 jit_solution(15200289475919762313)
XLA Ops:
  0.0 87.4 %moe_layer.1 = (f32[1024,768]{1,0:T(8,128)S(1)}, bf16[1024,256]{1,0:T(8,128)(2,1)S(1)}, bf16[256,768]{1,0:T(8,128)(2,1)S(1)}) custom-call(bf16[1024,768]{1,0:T(8,128)(2,1)} %bitcast.6, bf16[64,768]{1,0:T(8,128)(2,1)} %bitcast.7, s32[2,1024]{1,0:T(2,128)} %bitcast.8, s32[1,1024]{1,0:T(1,128)} %keep_hbm.1, bf16[2,768,3072]{2,1,0:T(8,128)(2,1)} %wi_hbm.1, ...), custom_call_target="tpu_custom_call" | custom-call | tf_op jit(solution)/shard_map/moe_layer/pallas_call | solution.py:257
  87.4 1.5 %finish.1 = bf16[1024,768]{1,0:T(8,128)(2,1)} custom-call(f32[1024,768]{1,0:T(8,128)S(1)} %get-tuple-element.8.acc, bf16[1024,256]{1,0:T(8,128)(2,1)S(1)} %get-tuple-element.9.last_cw, bf16[256,768]{1,0:T(8,128)(2,1)S(1)} %get-tuple-element.10.last_home), custom_call_target="tpu_custom_call" | custom-call | tf_op jit(solution)/shard_map/finish/pallas_call | solution.py:292
